TPU v7x, 64 devices: a 2x2x8 block of a 4x4x8 slice. The times are simulated.
64 devices in a mesh: dp: 4 (over x, y), cp: 16 (over z, core).
Axes of the slice: x: 2, y: 2, z: 8, core: 2. Of those that a mesh axis runs over, the one named last changes fastest.
The devices are a block of a 4x4x8 slice.
Arguments:
- x: bfloat16 [32, 5120], P('dp'), parts along dimension 0
- w_dq: bfloat16 [5120, 1536], replicated
- g_q: float32 [1536], replicated
- w_uq: bfloat16 [1536, 24576], replicated
- w_dkv: bfloat16 [5120, 576], replicated
- g_kv: float32 [512], replicated
- w_uk: bfloat16 [512, 128, 128], replicated
- w_uv: bfloat16 [512, 128, 128], replicated
- w_o: bfloat16 [16384, 5120], replicated
- cache_c: bfloat16 [32, 32768, 512], P('dp', 'cp'), parts along dimension 0
- cache_kr: bfloat16 [32, 32768, 64], P('dp', 'cp'), parts along dimension 0
- ctx_len: int32 [32], P('dp'), parts along dimension 0
Outputs:
- output 1: bfloat16 [32, 5120], P('dp'), parts along dimension 0
- output 2: bfloat16 [32, 512], P('dp'), parts along dimension 0
- output 3: bfloat16 [32, 64], P('dp'), parts along dimension 0
There are 4 independent parts. A program takes and returns all parts, laid end to end along the dimension named above; an argument that names none is the same for every part.
All inputs are finite; a program needn't handle non-finite values.
Results may differ from a plain program's by a relative error of at most 0.00631236.
Values sent between devices are 32-bit elements.
A program may use at most 768 MiB of HBM per device.

v0:
```python
import jax
import jax.numpy as jnp
from jax import lax
from jax.sharding import PartitionSpec as P, NamedSharding

NORM_EPS = 1e-6
ROPE_THETA = 10000.0
MASKED = -1e30


def rms_norm(values, gain_vec):
    mean_sq = jnp.mean(jnp.square(values), axis=-1, keepdims=True)
    return values * lax.rsqrt(mean_sq + NORM_EPS) * gain_vec


def rope_tables(positions, rope_dim):
    half_dim = rope_dim // 2
    inv_freq = ROPE_THETA ** (-2.0 * jnp.arange(half_dim, dtype=jnp.float32) / rope_dim)
    angles = positions.astype(jnp.float32)[..., None] * inv_freq
    return jnp.cos(angles), jnp.sin(angles)


def rope_rotate(values, cos_tab, sin_tab):
    half_dim = values.shape[-1] // 2
    lo_half = values[..., :half_dim]
    hi_half = values[..., half_dim:]
    return jnp.concatenate([lo_half * cos_tab - hi_half * sin_tab, hi_half * cos_tab + lo_half * sin_tab], axis=-1)


def project_step(x, w_dq, g_q, w_uq, w_dkv, g_kv, w_uk, ctx_len):
    n_req = x.shape[0]
    latent, n_heads, nope_dim = w_uk.shape
    rope_dim = w_dkv.shape[1] - latent
    cq_low = jnp.dot(x, w_dq, preferred_element_type=jnp.float32).astype(jnp.bfloat16)
    cq_norm = rms_norm(cq_low.astype(jnp.float32), g_q).astype(jnp.bfloat16)
    q_full = jnp.dot(cq_norm, w_uq, preferred_element_type=jnp.float32).astype(jnp.bfloat16)
    q_full = q_full.reshape(n_req, n_heads, nope_dim + rope_dim)
    cos_tab, sin_tab = rope_tables(ctx_len, rope_dim)
    q_rope = rope_rotate(q_full[:, :, nope_dim:].astype(jnp.float32), cos_tab[:, None, :], sin_tab[:, None, :]).astype(jnp.bfloat16)
    q_lat = jnp.einsum('bhn,khn->bhk', q_full[:, :, :nope_dim], w_uk, preferred_element_type=jnp.float32).astype(jnp.bfloat16)
    kv_full = jnp.dot(x, w_dkv, preferred_element_type=jnp.float32)
    c_new = rms_norm(kv_full[:, :latent], g_kv).astype(jnp.bfloat16)
    kr_new = rope_rotate(kv_full[:, latent:], cos_tab, sin_tab).astype(jnp.bfloat16)
    return q_lat, q_rope, c_new, kr_new


def block_partials(q_lat, q_rope, c_new, kr_new, cache_c, cache_kr, ctx_len, shard_idx, score_scale):
    t_dev = cache_c.shape[1]
    scores = (jnp.einsum('bhk,btk->bht', q_lat, cache_c, preferred_element_type=jnp.float32)
              + jnp.einsum('bhr,btr->bht', q_rope, cache_kr, preferred_element_type=jnp.float32)) * score_scale
    positions = shard_idx * t_dev + jnp.arange(t_dev)
    valid_pos = positions[None, None, :] < ctx_len[:, None, None]
    scores = jnp.where(valid_pos, scores, MASKED)
    is_owner = ((ctx_len // t_dev) == shard_idx)[:, None]
    new_score = (jnp.einsum('bhk,bk->bh', q_lat, c_new, preferred_element_type=jnp.float32)
                 + jnp.einsum('bhr,br->bh', q_rope, kr_new, preferred_element_type=jnp.float32)) * score_scale
    new_score = jnp.where(is_owner, new_score, MASKED)
    row_max = jnp.maximum(jnp.max(scores, axis=2), new_score)
    weights = jnp.where(valid_pos, jnp.exp(scores - row_max[:, :, None]), 0.0)
    new_weight = jnp.where(is_owner, jnp.exp(new_score - row_max), 0.0)
    row_sum = jnp.sum(weights, axis=2) + new_weight
    lat_acc = jnp.einsum('bht,btk->bhk', weights.astype(jnp.bfloat16), cache_c, preferred_element_type=jnp.float32)
    lat_acc = lat_acc + new_weight.astype(jnp.bfloat16).astype(jnp.float32)[:, :, None] * c_new.astype(jnp.float32)[:, None, :]
    return row_max, row_sum, lat_acc


def output_step(x, o_lat, w_uv, w_o):
    o_heads = jnp.einsum('bhk,khv->bhv', o_lat, w_uv, preferred_element_type=jnp.float32).astype(jnp.bfloat16)
    attn_out = jnp.dot(o_heads.reshape(x.shape[0], -1), w_o, preferred_element_type=jnp.float32)
    return (x.astype(jnp.float32) + attn_out).astype(jnp.bfloat16)


def solution(mesh):
    def decode_step(x, w_dq, g_q, w_uq, w_dkv, g_kv, w_uk, w_uv, w_o, cache_c, cache_kr, ctx_len):
        score_scale = (w_uk.shape[2] + cache_kr.shape[2]) ** -0.5
        shard_idx = lax.axis_index('cp')
        q_lat, q_rope, c_new, kr_new = project_step(x, w_dq, g_q, w_uq, w_dkv, g_kv, w_uk, ctx_len)
        row_max, row_sum, lat_acc = block_partials(q_lat, q_rope, c_new, kr_new, cache_c, cache_kr, ctx_len, shard_idx, score_scale)
        packed = jnp.concatenate([row_max[:, :, None], row_sum[:, :, None], lat_acc], axis=2)
        gathered = lax.all_gather(packed, 'cp')
        block_max = gathered[:, :, :, 0]
        glob_max = jnp.max(block_max, axis=0)
        factor = jnp.exp(block_max - glob_max[None])
        mass_sum = jnp.sum(factor * gathered[:, :, :, 1], axis=0)
        lat_sum = jnp.sum(factor[:, :, :, None] * gathered[:, :, :, 2:], axis=0)
        o_lat = (lat_sum / mass_sum[:, :, None]).astype(jnp.bfloat16)
        return output_step(x, o_lat, w_uv, w_o), c_new, kr_new

    spec_rows = P('dp', None)
    spec_cache = P('dp', 'cp', None)
    in_specs = (spec_rows, P(), P(), P(), P(), P(), P(), P(), P(), spec_cache, spec_cache, P('dp'))
    out_specs = (spec_rows, spec_rows, spec_rows)
    return jax.shard_map(decode_step, mesh=mesh, in_specs=in_specs, out_specs=out_specs, check_vma=False)
```

profile of v0, /device:TPU:21, one launch (start us, length us, event | category | flops | bytes accessed | tf_op | source)
XLA Modules:
  0.0 404.5 jit_solution(2825651462407161009)
XLA Ops:
  7.3 0.5 multiply_power_fusion
  7.8 7.8 %multiply_reduce_fusion = (f32[8]{0:T(128)S(1)}, f32[8,1536]{1,0:T(8,128)S(1)}) fusion(bf16[8,5120]{1,0:T(8,128)(2,1)} %param.12, bf16[5120,1536]{1,0:T(8,128)(2,1)} %param.13), kind=kOutput, calls=%fused_computation.44 | convolution fusion | flops 125878264 | bytes 15859744 | tf_op jit(solution)/shard_map/dot_general | solution.py:34
  15.6 26.7 %convolution_convert_fusion = bf16[8,24576]{1,0:T(8,128)(2,1)S(1)} fusion(bf16[1536,24576]{1,0:T(8,128)(2,1)} %param.15, f32[8,1536]{1,0:T(8,128)S(1)} %get-tuple-element.14, f32[1536]{0:T(1024)S(1)} %copy-done.5, f32[8]{0:T(128)S(1)} %add_rsqrt_fusion.1), kind=kOutput, calls=%fused_computation.2 | convolution fusion | flops 604213248 | bytes 75946016 | tf_op jit(solution)/shard_map/dot_general | solution.py:36
  42.4 0.6 reshape.119
  43.1 0.5 convert_element_type.64
  43.6 0.5 fusion.42
  44.3 4.3 %fusion.49 = f32[8,576]{1,0:T(8,128)S(1)} fusion(bf16[8,5120]{1,0:T(8,128)(2,1)S(1)} %copy-done.4, bf16[5120,576]{0,1:T(8,128)(2,1)} %param.16), kind=kOutput, calls=%fused_computation.76 | convolution fusion | flops 47185920 | bytes 5998592 | tf_op jit(solution)/shard_map/dot_general | solution.py:41
  48.7 0.1 copy.55
  48.9 0.7 convert_element_type.63
  49.7 40.6 %fusion.17 = bf16[8,128,512]{2,0,1:T(8,128)(2,1)S(1)} fusion(bf16[512,128,128]{2,1,0:T(8,128)(2,1)} %param.18, bf16[8,128,128]{2,1,0:T(8,128)(2,1)S(1)} %slice.43), kind=kOutput, calls=%fused_computation.23 | convolution fusion | flops 134742016 | bytes 18087936 | tf_op jit(solution)/shard_map/bhn,khn->bhk/dot_general | solution.py:40
  90.3 0.4 fusion.29
  90.7 14.6 %fusion.31 = f32[8,128,2048]{2,1,0:T(8,128)} fusion(bf16[8,2048,512]{2,1,0:T(8,128)(2,1)} %param.21, bf16[8,128,512]{2,0,1:T(8,128)(2,1)S(1)} %fusion.17), kind=kOutput, calls=%fused_computation.29 | convolution fusion | flops 2147483648 | bytes 26214400 | tf_op jit(solution)/shard_map/bhk,btk->bht/dot_general | solution.py:49
  105.3 0.8 subtract_convert_fusion.1
  106.2 0.1 subtract_convert_fusion
  106.3 0.1 fusion.34
  106.5 5.2 %fusion.48 = (f32[8,128]{1,0:T(8,128)S(1)}, f32[8,128,2048]{2,1,0:T(8,128)S(1)}) fusion(f32[8,128,2048]{2,1,0:T(8,128)} %fusion.31, bf16[8,2048,64]{1,2,0:T(8,128)(2,1)S(1)} %copy-done, bf16[8,128,32]{1,2,0:T(8,128)(2,1)S(1)} %get-tuple-element.8, bf16[8,128,32]{1,2,0:T(8,128)(2,1)S(1)} %get-tuple-element.7, pred[8,2048]{1,0:T(8,128)(4,1)S(1)} %broadcast_compare_fusion), kind=kOutput, calls=%fused_computation.75 | convolution fusion | flops 277085184 | bytes 19025920 | tf_op jit(solution)/shard_map/bhr,btr->bht/dot_general | solution.py:50
  111.7 3.1 copy-done.2
  114.9 1.8 fusion.6
  116.8 0.2 copy.44
  117.0 0.2 copy.43
  117.2 10.8 %multiply_add_fusion = f32[8,128,512]{2,1,0:T(8,128)S(1)} fusion(bf16[8,2048,512]{2,1,0:T(8,128)(2,1)} %param.21, f32[8,128,2048]{2,1,0:T(8,128)} %copy-done.2, f32[8,128]{1,0:T(8,128)S(1)} %fusion.43, pred[8,2048]{1,0:T(8,128)(4,1)S(1)} %broadcast_compare_fusion, f32[8,512]{1,0:T(8,128)S(1)} %get-tuple-element.5, f32[8,128]{1,0:T(8,128)S(1)} %convert_element_type.99), kind=kOutput, calls=%fused_computation.21 | convolution fusion | flops 2154823680 | bytes 27303936 | tf_op jit(solution)/shard_map/bht,btk->bhk/dot_general | solution.py:62
  128.1 2.5 pad_maximum_fusion
  130.6 3.4 copy.45
  134.0 0.7 pad_maximum_fusion.4
  134.7 183.2 %all-gather.3.cloned.1.call-done = f32[128,128,514]{1,0,2:T(8,128)} async-done(((f32[8,128,514]{1,0,2:T(8,128)}), f32[128,128,514]{1,0,2:T(8,128)}) %all-gather.3.cloned.1.call-update) | async-done | bytes 33685520 | tf_op jit(solution)/shard_map/all_gather | solution.py:80
  317.9 0.9 slice_reduce_fusion
  318.7 0.9 fusion.36
  319.6 0.9 exponential_bitcast_fusion
  320.5 13.4 %fusion = f32[8,128,512]{1,0,2:T(8,128)S(1)} fusion(f32[16,8,128,514]{2,1,0,3:T(8,128)} %bitcast.53, f32[16,8,128]{2,1,0:T(8,128)S(1)} %exponential_bitcast_fusion), kind=kLoop, calls=%fused_computation.1 | loop fusion | flops 16252928 | bytes 35717120 | tf_op jit(solution)/shard_map/reduce_sum | solution.py:85
  333.9 1.9 copy.53
  335.9 1.8 divide_convert_fusion
  337.7 59.7 %fusion.7 = bf16[8,5120]{1,0:T(8,128)(2,1)} fusion(bf16[16384,5120]{1,0:T(8,128)(2,1)} %param.20, bf16[8,5120]{1,0:T(8,128)(2,1)S(1)} %copy-done.4, bf16[512,128,128]{2,1,0:T(8,128)(2,1)} %param.19, bf16[8,128,512]{2,1,0:T(8,128)(2,1)S(1)} %divide_convert_fusion), kind=kOutput, calls=%fused_computation.12 | convolution fusion | flops 1476648960 | bytes 185761792 | tf_op jit(solution)/shard_map/dot_general | solution.py:69
  (33 shorter events, 0.8 us)
Async XLA Ops:
  7.2 99.3 %copy-start = (bf16[8,2048,64]{1,2,0:T(8,128)(2,1)S(1)}, bf16[8,2048,64]{1,2,0:T(8,128)(2,1)}, u32[]{:S(2)}) copy-start(bf16[8,2048,64]{1,2,0:T(8,128)(2,1)} %param.22) | copy-start | bytes 6291460
  7.2 310.7 %all-gather.3.cloned.1.call-start = ((), (), s32[]{:S(2)}) async-start(), calls=%async_computation | async-start | bytes 35790848 | tf_op jit(solution)/shard_map/all_gather | solution.py:80
  7.8 7.8 %copy-start.5 = (f32[1536]{0:T(1024)S(1)}, f32[1536]{0:T(1024)}, u32[]{:S(2)}) copy-start(f32[1536]{0:T(1024)} %param.14) | copy-start | bytes 18436
  15.6 27.5 %copy-start.9 = (s32[8]{0:T(128)S(1)}, s32[8]{0:T(128)}, u32[]{:S(2)}) copy-start(s32[8]{0:T(128)} %param.23) | copy-start | bytes 100
  15.6 28.6 %copy-start.4 = (bf16[8,5120]{1,0:T(8,128)(2,1)S(1)}, bf16[8,5120]{1,0:T(8,128)(2,1)}, u32[]{:S(2)}) copy-start(bf16[8,5120]{1,0:T(8,128)(2,1)} %param.12) | copy-start | bytes 245764
  42.4 7.2 %copy-start.7 = (f32[512]{0:T(512)S(1)}, f32[512]{0:T(512)}, u32[]{:S(2)}) copy-start(f32[512]{0:T(512)} %param.17) | copy-start | bytes 6148
  49.7 40.6 %copy-start.6 = (bf16[8,512]{1,0:T(8,128)(2,1)}, bf16[8,512]{1,0:T(8,128)(2,1)S(1)}, u32[]{:S(2)}) copy-start(bf16[8,512]{1,0:T(8,128)(2,1)S(1)} %get-tuple-element.6) | copy-start | bytes 24580
  90.7 15.5 %copy-start.3 = (f32[8,128,64]{1,2,0:T(8,128)S(1)}, f32[8,128,64]{1,2,0:T(8,128)}, u32[]{:S(2)}) copy-start(f32[8,128,64]{1,2,0:T(8,128)} %convert_element_type.63) | copy-start | bytes 786436
  106.5 5.2 %copy-start.8 = (pred[8]{0:T(512)(128)(4,1)S(1)}, pred[8]{0:T(512)(128)(4,1)}, u32[]{:S(2)}) copy-start(pred[8]{0:T(512)(128)(4,1)} %fusion.42) | copy-start | bytes 28
  111.6 3.2 copy-start.2
  337.7 59.8 %copy-start.1 = (bf16[8,2048,64]{1,2,0:T(8,128)(2,1)S(1)}, bf16[8,2048,64]{1,2,0:T(8,128)(2,1)}, u32[]{:S(2)}) copy-start(bf16[8,2048,64]{1,2,0:T(8,128)(2,1)} %param.22) | copy-start | bytes 6291460
Sparse Core Ops, SparseCore 0:
  134.2 183.6 all-gather.2
where the time goes:
time: 409 us; the launch traced here: 404 us
  waiting for transfers between devices  183 us (45%)
  matrix products  170 us (42%)
  other arithmetic  26.6 us (7%)
  between operations  14.5 us (4%)
  local copies, waits for them, and re-layouts  9.79 us (2%)
    all_gather x1, waiting for transfers between devices, decode_step(): gathered = lax.all_gather(packed, 'cp')  183 us
    dot_general x1, matrix products, output_step(): jnp.dot(o_heads.reshape(x.shape[0], -1), w_o, preferred_element_type=jnp....  59.7 us
    dot_general x1, matrix products, project_step(): jnp.einsum('bhn,khn->bhk', q_full[:, :, :nope_dim], w_uk, preferred_eleme...  40.6 us
    dot_general x1, matrix products, project_step(): jnp.dot(cq_norm, w_uq, preferred_element_type=jnp.float32)  26.7 us
    dot_general x1, matrix products, block_partials(): jnp.einsum('bhk,btk->bht', q_lat, cache_c, preferred_element_type=jnp.flo...  14.6 us
    reduce_sum x1, other arithmetic, decode_step(): lat_sum = jnp.sum(factor[:, :, :, None] * gathered[:, :, :, 2:], axis=0)  13.4 us
    dot_general x1, matrix products, block_partials(): jnp.einsum('bht,btk->bhk', weights.astype(jnp.bfloat16), cache_c, preferr...  10.8 us
  transfers between devices with their start and end apart: 1, of which 1 were waited for; matrix products, arithmetic and copies ran while one was open for 0% of the time, Pallas kernels for 0%

commit v1 on v0

v1 whole, which is shorter than its diff:
```python
import functools

import jax
import jax.numpy as jnp
from jax import lax
from jax.experimental import pallas as pl
from jax.experimental.pallas import tpu as pltpu
from jax.sharding import PartitionSpec as P

NORM_EPS = 1e-6
ROPE_THETA = 10000.0
LANES = 128
LOWEST = float(jnp.finfo(jnp.float32).min)
MESH = pl.DeviceIdType.MESH


def rms_norm(values, gain_vec):
    mean_sq = jnp.mean(jnp.square(values), axis=-1, keepdims=True)
    return values * lax.rsqrt(mean_sq + NORM_EPS) * gain_vec


def rope_tables(positions, rope_dim):
    half_dim = rope_dim // 2
    inv_freq = ROPE_THETA ** (-2.0 * jnp.arange(half_dim, dtype=jnp.float32) / rope_dim)
    angles = positions.astype(jnp.float32)[..., None] * inv_freq
    return jnp.cos(angles), jnp.sin(angles)


def rope_rotate(values, cos_tab, sin_tab):
    half_dim = values.shape[-1] // 2
    lo_half = values[..., :half_dim]
    hi_half = values[..., half_dim:]
    return jnp.concatenate([lo_half * cos_tab - hi_half * sin_tab, hi_half * cos_tab + lo_half * sin_tab], axis=-1)


def latent_step(x, w_dq, g_q, w_dkv, g_kv, ctx_len):
    latent = g_kv.shape[0]
    rope_dim = w_dkv.shape[1] - latent
    cq_low = jnp.dot(x, w_dq, preferred_element_type=jnp.float32).astype(jnp.bfloat16)
    cq_norm = rms_norm(cq_low.astype(jnp.float32), g_q).astype(jnp.bfloat16)
    cos_tab, sin_tab = rope_tables(ctx_len, rope_dim)
    kv_full = jnp.dot(x, w_dkv, preferred_element_type=jnp.float32)
    c_new = rms_norm(kv_full[:, :latent], g_kv).astype(jnp.bfloat16)
    kr_new = rope_rotate(kv_full[:, latent:], cos_tab, sin_tab).astype(jnp.bfloat16)
    return cq_norm, cos_tab, sin_tab, c_new, kr_new


def head_queries(cq_norm, w_uq, w_uk, cos_tab, sin_tab):
    n_req = cq_norm.shape[0]
    n_heads, nope_dim = w_uk.shape[1:]
    q_full = jnp.dot(cq_norm, w_uq, preferred_element_type=jnp.float32).astype(jnp.bfloat16)
    q_full = q_full.reshape(n_req, n_heads, -1)
    q_rope = rope_rotate(q_full[:, :, nope_dim:].astype(jnp.float32), cos_tab[:, None, :], sin_tab[:, None, :])
    q_lat = jnp.einsum('bhn,khn->bhk', q_full[:, :, :nope_dim], w_uk, preferred_element_type=jnp.float32)
    return q_lat.astype(jnp.bfloat16), q_rope.astype(jnp.bfloat16)


def merge(left, right, latent):
    half = LANES // 2
    m_l, m_r = left[:, latent:latent + 1], right[:, latent:latent + 1]
    l_l, l_r = left[:, latent + half:latent + half + 1], right[:, latent + half:latent + half + 1]
    top = jnp.maximum(m_l, m_r)
    f_l, f_r = jnp.exp(m_l - top), jnp.exp(m_r - top)
    acc = left[:, :latent] * f_l + right[:, :latent] * f_r
    return acc, top, l_l * f_l + l_r * f_r


def put_block(ref, index, acc, top, mass):
    latent = acc.shape[-1]
    rows = acc.shape[0]
    shape = ref.at[index].shape
    half = LANES // 2
    ref[index + (slice(None),) * (len(shape) - 1) + (slice(0, latent),)] = acc.reshape(shape[:-1] + (latent,))
    stats = jnp.where(lax.broadcasted_iota(jnp.int32, (rows, LANES), 1) < half, top, mass)
    ref[index + (slice(None),) * (len(shape) - 1) + (slice(latent, latent + LANES),)] = stats.reshape(shape[:-1] + (LANES,))


def attend_kernel(nz, scale, ctx_ref, q_ref, cn_ref, kn_ref, c_hbm, k_hbm, out_ref,
                  c_buf, k_buf, q_all, s_buf, own, other, mine, chain, hop_out,
                  c_sem, k_sem, q_recv, q_send, q_send_x, x_send, x_recv, h_send, h_recv):
    n_req, t_dev, latent = c_buf.shape
    rope_dim = k_buf.shape[1]
    per = q_ref.shape[1]
    n_dev = 2 * nz
    heads = n_dev * per
    far = nz // 2
    me = lax.axis_index('cp')
    z, core = me // 2, me % 2
    partner = me + 1 - 2 * core
    at = lambda off: lax.rem(z + off + nz, nz)
    sides = (at(1) * 2 + core, at(-1) * 2 + core)
    hops_from = (lambda off: at(-off) * 2 + core, lambda off: at(off) * 2 + core)

    def remote(src, dst, send, recv, target):
        return pltpu.make_async_remote_copy(src_ref=src, dst_ref=dst, send_sem=send, recv_sem=recv,
                                            device_id={'cp': target}, device_id_type=MESH)

    for r in range(n_req):
        pltpu.make_async_copy(c_hbm.at[r], c_buf.at[r], c_sem.at[r]).start()
        pltpu.make_async_copy(k_hbm.at[r], k_buf.at[r], k_sem.at[r]).start()

    barrier = pltpu.get_barrier_semaphore()
    for peer in (*sides, partner):
        pl.semaphore_signal(barrier, inc=1, device_id={'cp': peer}, device_id_type=MESH)
    q_all[:, pl.ds(me, 1)] = q_ref[...].reshape(n_req, 1, per, latent + LANES)
    pl.semaphore_wait(barrier, 3)

    def ring_copy(r, hop, way, src_dev):
        src = q_ref.at[r] if hop == 1 else q_all.at[r, src_dev]
        return remote(src, q_all.at[r, src_dev], q_send.at[r, hop - 1, way], q_recv.at[r, src_dev], sides[way])

    def cross_copy(r, slot, src_dev):
        src = q_ref.at[r] if slot == 0 else q_all.at[r, src_dev]
        return remote(src, q_all.at[r, src_dev], q_send_x.at[r, slot], q_recv.at[r, src_dev], partner)

    def arrived(r, src_dev):
        remote(q_all.at[r, src_dev], q_all.at[r, src_dev], q_send.at[r, 0, 0], q_recv.at[r, src_dev], partner).wait_recv()

    def gather_hop(r, hop):
        if hop == 1:
            for way in range(2):
                ring_copy(r, hop, way, me).start()
            cross_copy(r, 0, me).start()
            return
        for way in range(2):
            src_dev = hops_from[way](hop - 1)

            def forward(way=way, src_dev=src_dev):
                arrived(r, src_dev)
                if hop <= far:
                    if hop == far:
                        @pl.when(core == way)
                        def _():
                            ring_copy(r, hop, way, src_dev).start()
                    else:
                        ring_copy(r, hop, way, src_dev).start()
                cross_copy(r, 2 * (hop - 2) + way + 1 if hop <= far else 2 * far - 1, src_dev).start()

            if hop == far + 1:
                pl.when(core == way)(forward)
            else:
                forward()

    def attend(r):
        def from_partner(d, carry):
            arrived(r, d * 2 + 1 - core)
            return carry
        lax.fori_loop(0, nz, from_partner, 0)
        pltpu.make_async_copy(c_hbm.at[r], c_buf.at[r], c_sem.at[r]).wait()
        pltpu.make_async_copy(k_hbm.at[r], k_buf.at[r], k_sem.at[r]).wait()
        q = q_all[r].reshape(heads, latent + LANES)
        q_lat = q[:, :latent].astype(jnp.bfloat16)
        q_rope = q[:, latent:latent + rope_dim].astype(jnp.bfloat16)
        n = ctx_ref[r]
        base = me * t_dev
        step = 512
        top = jnp.full((heads, LANES), LOWEST, jnp.float32)

        def valid(t0):
            return base + t0 + lax.broadcasted_iota(jnp.int32, (1, step), 1) < n

        for t0 in range(0, t_dev, step):
            s = lax.dot_general(q_lat, c_buf[r, t0:t0 + step, :], (((1,), (1,)), ((), ())), preferred_element_type=jnp.float32)
            s += jnp.dot(q_rope, k_buf[r, :, t0:t0 + step], preferred_element_type=jnp.float32)
            s = jnp.where(valid(t0), s * scale, LOWEST)
            s_buf[:, t0:t0 + step] = s
            for j in range(0, step, LANES):
                top = jnp.maximum(top, s[:, j:j + LANES])
        c_new = cn_ref[r]
        kr_new = kn_ref[r]
        s_new = (jnp.sum(q_lat.astype(jnp.float32) * c_new, axis=1, keepdims=True)
                 + jnp.sum(q_rope.astype(jnp.float32) * kr_new, axis=1, keepdims=True)) * scale
        owner = jnp.logical_and(n >= base, n < base + t_dev)
        s_new = jnp.where(owner, s_new, LOWEST)
        m = jnp.maximum(jnp.max(top, axis=1, keepdims=True), s_new)
        w_new = jnp.where(owner, jnp.exp(s_new - m), 0.0)
        mass = jnp.zeros((heads, LANES), jnp.float32)
        acc = w_new.astype(jnp.bfloat16).astype(jnp.float32) * c_new
        for t0 in range(0, t_dev, step):
            w = jnp.where(valid(t0), jnp.exp(s_buf[:, t0:t0 + step] - m), 0.0)
            for j in range(0, step, LANES):
                mass += w[:, j:j + LANES]
            acc += jnp.dot(w.astype(jnp.bfloat16), c_buf[r, t0:t0 + step, :], preferred_element_type=jnp.float32)
        put_block(own, (r,), acc, m, jnp.sum(mass, axis=1, keepdims=True) + w_new)

    def cross_sum(r):
        return remote(own.at[r, :, 1 - core], other.at[r], x_send.at[r], x_recv.at[r], partner)

    def chain_copy(r, hop, way, src):
        return remote(src, chain.at[r, hop - 1, way], h_send.at[r, hop - 1, way], h_recv.at[r, hop - 1, way], sides[way])

    def flat(block):
        return block.reshape(-1, latent + LANES)

    def reduce_hop(r, hop):
        if hop == 1:
            cross_sum(r).wait_recv()
            put_block(mine, (r,), *merge(flat(own[r, :, core]), flat(other[r]), latent))
        for way in range(2):
            dest = at((far + 1 - hop) * (1 - 2 * way))
            if hop == 1:
                @pl.when(core == way)
                def _(way=way, dest=dest):
                    chain_copy(r, hop, way, mine.at[r, dest]).start()
                continue

            def pass_on(way=way, dest=dest):
                chain_copy(r, hop - 1, way, chain.at[r, hop - 2, way]).wait_recv()
                put_block(hop_out, (r, hop - 2, way), *merge(chain[r, hop - 2, way], mine[r, dest], latent))
                chain_copy(r, hop, way, hop_out.at[r, hop - 2, way]).start()

            if hop == 2:
                pl.when(core == way)(pass_on)

                @pl.when(core != way)
                def _(way=way, dest=dest):
                    chain_copy(r, hop, way, mine.at[r, dest]).start()
            else:
                pass_on()

    def finish(r):
        for way in range(2):
            chain_copy(r, far, way, chain.at[r, far - 1, way]).wait_recv()
        acc, top, mass = merge(chain[r, far - 1, 0], chain[r, far - 1, 1], latent)
        stats = jnp.where(lax.broadcasted_iota(jnp.int32, (per, LANES), 1) < LANES // 2, top, mass)
        both = jnp.concatenate([acc, stats], axis=1)
        acc, top, mass = merge(both, mine[r, z], latent)
        out_ref[r] = (acc / mass).astype(out_ref.dtype)

    def slot(s, carry):
        def at_slot(delay, body):
            r = s - delay

            @pl.when(jnp.logical_and(r >= 0, r < n_req))
            def _():
                body(r)

        for hop in range(far + 1, 0, -1):
            at_slot(hop - 1, functools.partial(gather_hop, hop=hop))
        at_slot(2 * far + 2, finish)
        for hop in range(far, 0, -1):
            at_slot(far + 1 + hop, functools.partial(reduce_hop, hop=hop))

        def compute(r):
            attend(r)
            cross_sum(r).start()
        at_slot(far + 1, compute)
        return carry

    lax.fori_loop(0, n_req + 2 * far + 2, slot, 0)

    def drain(r, carry):
        for way in range(2):
            for hop in range(1, far + 1):
                def ring_done(way=way, hop=hop):
                    ring_copy(r, hop, way, me).wait_send()

                def chain_done(way=way, hop=hop):
                    chain_copy(r, hop, way, mine.at[r, 0]).wait_send()
                pl.when(core == way)(ring_done) if hop == far else ring_done()
                pl.when(core == way)(chain_done) if hop == 1 else chain_done()
        for slot_x in range(nz):
            cross_copy(r, slot_x, me).wait_send()
        cross_sum(r).wait_send()
        return carry
    lax.fori_loop(0, n_req, drain, 0)


def attend_blocks(nz, ctx_len, q_own, c_new, kr_new, cache_c, cache_krt, scale):
    n_req, per, width = q_own.shape
    _, t_dev, latent = cache_c.shape
    rope_dim = cache_krt.shape[1]
    far = nz // 2
    heads = 2 * nz * per
    vmem = pl.BlockSpec(memory_space=pltpu.VMEM)
    hbm = pl.BlockSpec(memory_space=pl.ANY)
    dma = pltpu.SemaphoreType.DMA
    f32 = jnp.float32
    return pl.pallas_call(
        functools.partial(attend_kernel, nz, scale),
        out_shape=jax.ShapeDtypeStruct((n_req, per, latent), jnp.bfloat16),
        in_specs=[pl.BlockSpec(memory_space=pltpu.SMEM), vmem, vmem, vmem, hbm, hbm],
        out_specs=vmem,
        scratch_shapes=[
            pltpu.VMEM((n_req, t_dev, latent), jnp.bfloat16),
            pltpu.VMEM((n_req, rope_dim, t_dev), jnp.bfloat16),
            pltpu.VMEM((n_req, 2 * nz, per, width), f32),
            pltpu.VMEM((heads, t_dev), f32),
            pltpu.VMEM((n_req, nz, 2, per, width), f32),
            pltpu.VMEM((n_req, nz, per, width), f32),
            pltpu.VMEM((n_req, nz, per, width), f32),
            pltpu.VMEM((n_req, far, 2, per, width), f32),
            pltpu.VMEM((n_req, far - 1, 2, per, width), f32),
            dma((n_req,)),
            dma((n_req,)),
            dma((n_req, 2 * nz)),
            dma((n_req, far, 2)),
            dma((n_req, nz)),
            dma((n_req,)),
            dma((n_req,)),
            dma((n_req, far, 2)),
            dma((n_req, far, 2)),
        ],
        compiler_params=pltpu.CompilerParams(collective_id=0, has_side_effects=True, vmem_limit_bytes=56 * 2 ** 20),
        name='attend_blocks',
    )(ctx_len, q_own, c_new, kr_new, cache_c, cache_krt)


def add_up_kernel(nz, part_ref, x_ref, out_ref, got, mine, theirs, total, a_send, a_recv, x_send, x_recv, b_send, b_recv):
    me = lax.axis_index('cp')
    z, core = me // 2, me % 2
    partner = me + 1 - 2 * core
    width = mine.shape[1]
    at = lambda off: lax.rem(z + off, nz)
    cols = lambda piece: pl.ds(pl.multiple_of(piece * width, LANES), width)

    def remote(src, dst, send, recv, target):
        return pltpu.make_async_remote_copy(src_ref=src, dst_ref=dst, send_sem=send, recv_sem=recv,
                                            device_id={'cp': target}, device_id_type=MESH)

    barrier = pltpu.get_barrier_semaphore()
    for off in range(1, nz):
        pl.semaphore_signal(barrier, inc=1, device_id={'cp': at(off) * 2 + core}, device_id_type=MESH)
    pl.semaphore_signal(barrier, inc=1, device_id={'cp': partner}, device_id_type=MESH)
    pl.semaphore_wait(barrier, nz)
    order = sorted(range(1, nz), key=lambda off: -min(off, nz - off))
    scatter = {off: remote(part_ref.at[:, cols(at(off))], got.at[off - 1], a_send.at[off - 1], a_recv.at[off - 1], at(off) * 2 + core) for off in order}
    for off in order:
        scatter[off].start()
    acc = part_ref[:, cols(z)]
    for off in reversed(order):
        scatter[off].wait_recv()
        acc += got[off - 1]
    mine[...] = acc
    swap = remote(mine, theirs, x_send, x_recv, partner)
    swap.start()
    swap.wait_recv()
    total[z] = mine[...] + theirs[...]
    spread = {off: remote(total.at[z], total.at[z], b_send.at[off - 1], b_recv.at[off - 1], at(off) * 2 + core) for off in order}
    for off in order:
        spread[off].start()
    for off in reversed(order):
        src = at(nz - off)
        remote(total.at[src], total.at[src], b_send.at[off - 1], b_recv.at[off - 1], at(off) * 2 + core).wait_recv()
    for piece in range(nz):
        span = slice(piece * width, (piece + 1) * width)
        out_ref[:, span] = (x_ref[:, span].astype(jnp.float32) + total[piece]).astype(out_ref.dtype)
    swap.wait_send()
    for off in order:
        scatter[off].wait_send()
        spread[off].wait_send()


def add_up(nz, part, x):
    rows, columns = part.shape
    width = columns // nz
    vmem = pl.BlockSpec(memory_space=pltpu.VMEM)
    dma = pltpu.SemaphoreType.DMA
    return pl.pallas_call(
        functools.partial(add_up_kernel, nz),
        out_shape=jax.ShapeDtypeStruct((rows, columns), x.dtype),
        in_specs=[vmem, vmem],
        out_specs=vmem,
        scratch_shapes=[
            pltpu.VMEM((nz - 1, rows, width), jnp.float32),
            pltpu.VMEM((rows, width), jnp.float32),
            pltpu.VMEM((rows, width), jnp.float32),
            pltpu.VMEM((nz, rows, width), jnp.float32),
            dma((nz - 1,)), dma((nz - 1,)), dma, dma, dma((nz - 1,)), dma((nz - 1,)),
        ],
        compiler_params=pltpu.CompilerParams(collective_id=1, has_side_effects=True),
        name='add_up',
    )(part, x)


def solution(mesh):
    n_cp = mesh.shape['cp']
    nz = n_cp // 2

    def decode_step(x, w_dq, g_q, w_uq, w_dkv, g_kv, w_uk, w_uv, w_o, cache_c, cache_kr, ctx_len):
        latent, n_heads, nope_dim = w_uk.shape
        n_req = x.shape[0]
        rope_dim = cache_kr.shape[2]
        per = n_heads // n_cp
        scale = (nope_dim + rope_dim) ** -0.5
        shard_idx = lax.axis_index('cp')
        cut = lambda w, axis, size: lax.dynamic_slice_in_dim(w, shard_idx * size, size, axis)
        cq_norm, cos_tab, sin_tab, c_new, kr_new = latent_step(x, w_dq, g_q, w_dkv, g_kv, ctx_len)
        q_lat, q_rope = head_queries(cq_norm, cut(w_uq, 1, per * (nope_dim + rope_dim)), cut(w_uk, 1, per), cos_tab, sin_tab)
        pad = jnp.zeros((n_req, per, LANES - rope_dim), jnp.float32)
        q_own = jnp.concatenate([q_lat.astype(jnp.float32), q_rope.astype(jnp.float32), pad], axis=2)
        o_lat = attend_blocks(nz, ctx_len, q_own, c_new.astype(jnp.float32)[:, None], kr_new.astype(jnp.float32)[:, None],
                              cache_c, cache_kr.transpose(0, 2, 1), scale)
        o_heads = jnp.einsum('bhk,khv->bhv', o_lat, cut(w_uv, 1, per), preferred_element_type=jnp.float32).astype(jnp.bfloat16)
        part = jnp.dot(o_heads.reshape(n_req, -1), cut(w_o, 0, per * w_uv.shape[2]), preferred_element_type=jnp.float32)
        return add_up(nz, part, x), c_new, kr_new

    spec_rows = P('dp', None)
    spec_cache = P('dp', 'cp', None)
    in_specs = (spec_rows, P(), P(), P(), P(), P(), P(), P(), P(), spec_cache, spec_cache, P('dp'))
    out_specs = (spec_rows, spec_rows, spec_rows)
    return jax.shard_map(decode_step, mesh=mesh, in_specs=in_specs, out_specs=out_specs, check_vma=False)
```

time: 409 us -> 123 us (0.30); the launches traced: 404 us -> 123 us
  waiting for transfers between devices: 183 us -> 0 us
  matrix products: 170 us -> 21.9 us
  Pallas kernels: 0 us -> 93.3 us
  other arithmetic: 26.6 us -> 2.54 us
  between operations: 14.5 us -> 0.79 us
  local copies, waits for them, and re-layouts: 9.79 us -> 4.1 us
    all_gather x1 -> x0, waiting for transfers between devices: 183 us -> none  [decode_step(): gathered = lax.all_gather(packed, 'cp')]
    dot_general x10 -> x5, matrix products: 170 us -> 21.9 us  [the longest x1 7.77 us: latent_step(): jnp.dot(x, w_dq, preferred_element_type=jnp.float32).astype(jnp.bfloat16)]
    pallas_call x0 -> x2, Pallas kernels: none -> 93.3 us  [the longest x1 72 us: attend_blocks(): pl.pallas_call(functools.partial(attend_kernel, nz, scale), out_shape=jax...]
    reduce_sum x3 -> x0, other arithmetic: 16.1 us -> none  [the longest x1 13.4 us: decode_step(): lat_sum = jnp.sum(factor[:, :, :, None] * gathered[:, :, :, 2:], axis=0)]
  transfers between devices with their start and end apart: 1 -> 0, of which waited for: 1 -> 0; matrix products, arithmetic and copies ran while one was open for 0% -> 0% of each run, Pallas kernels for 0% -> 0%
where the time goes in v1:
time: 123 us
  Pallas kernels  93.3 us (76%)
  matrix products  21.9 us (18%)
  local copies, waits for them, and re-layouts  4.1 us (3%)
  other arithmetic  2.54 us (2%)
    pallas_call x1, Pallas kernels, attend_blocks(): pl.pallas_call(functools.partial(attend_kernel, nz, scale), out_shape=jax...  72 us
    pallas_call x1, Pallas kernels, add_up(): pl.pallas_call(functools.partial(add_up_kernel, nz), out_shape=jax.ShapeD...  21.3 us
    dot_general x1, matrix products, latent_step(): jnp.dot(x, w_dq, preferred_element_type=jnp.float32).astype(jnp.bfloat16)  7.77 us
    dot_general x1, matrix products, decode_step(): jnp.dot(o_heads.reshape(n_req, -1), cut(w_o, 0, per * w_uv.shape[2]), pre...  6.34 us
    dot_general x1, matrix products, latent_step(): kv_full = jnp.dot(x, w_dkv, preferred_element_type=jnp.float32)  4.29 us
    dot_general x1, matrix products, head_queries(): jnp.dot(cq_norm, w_uq, preferred_element_type=jnp.float32)  3.1 us

profile of v1, /device:TPU:21, one launch (start us, length us, event | category | flops | bytes accessed | tf_op | source)
XLA Modules:
  0.0 122.6 jit_solution(9409207372449705559)
XLA Ops:
  0.6 0.0 copy-start.2
  0.6 0.0 copy-start
  0.7 1.7 %constant_dynamic-slice_fusion = (bf16[512,8,128]{2,1,0:T(8,128)(2,1)S(1)}, bf16[512,8,128]{2,1,0:T(8,128)(2,1)S(1)}) fusion(bf16[512,128,128]{2,1,0:T(8,128)(2,1)} %param.18, s32[]{:T(128)S(6)} %select_n.10, bf16[512,128,128]{2,1,0:T(8,128)(2,1)} %param.19), kind=kLoop, calls=%fused_computation.35 | loop fusion | bytes 4194308 | tf_op jit(solution)/shard_map/dynamic_slice | solution.py:387
  2.4 0.0 copy-start.4
  2.4 0.0 copy-start.3
  2.4 7.8 %multiply_reduce_fusion = (f32[8]{0:T(128)S(1)}, f32[8,1536]{1,0:T(8,128)S(1)}) fusion(bf16[8,5120]{1,0:T(8,128)(2,1)} %x_ref.1, bf16[5120,1536]{1,0:T(8,128)(2,1)} %param.13), kind=kOutput, calls=%fused_computation.17 | convolution fusion | flops 125878264 | bytes 15859744 | tf_op jit(solution)/shard_map/dot_general | solution.py:39
  10.2 0.0 copy-done.2
  10.2 3.1 %fusion.4 = bf16[8,1536]{1,0:T(8,128)(2,1)S(1)} fusion(bf16[1536,24576]{1,0:T(8,128)(2,1)} %param.15, s32[]{:T(128)S(6)} %select_n.11, f32[8,1536]{1,0:T(8,128)S(1)} %get-tuple-element.10, f32[1536]{0:T(1024)S(1)} %copy-done.2, f32[8]{0:T(128)S(1)} %add_rsqrt_fusion.1), kind=kOutput, calls=%fused_computation.4 | convolution fusion | flops 37797888 | bytes 4798500 | tf_op jit(solution)/shard_map/dot_general | solution.py:51
  13.3 0.1 reshape.114
  13.4 0.0 copy-done
  13.4 4.3 %fusion.21 = f32[8,576]{1,0:T(8,128)S(1)} fusion(bf16[8,5120]{1,0:T(8,128)(2,1)S(1)} %copy-done, bf16[5120,576]{0,1:T(8,128)(2,1)} %param.16), kind=kOutput, calls=%fused_computation.40 | convolution fusion | flops 47185920 | bytes 5998592 | tf_op jit(solution)/shard_map/dot_general | solution.py:42
  17.8 0.0 copy-done.4
  17.8 0.1 subtract_convert_fusion.1
  17.9 0.1 subtract_convert_fusion
  18.0 0.1 maximum_convert_fusion
  18.1 0.4 fusion.9
  18.5 0.1 pad.6.clone
  18.6 0.7 maximum_maximum_fusion.q_ref
  19.3 0.1 multiply_reduce_fusion.1
  19.4 0.0 copy-done.3
  19.4 0.1 multiply_convert_fusion.2
  19.5 0.0 copy-start.1
  19.5 0.6 reshape.116.cn_ref
  20.1 0.7 maximum_convert_fusion.1.kn_ref
  20.8 72.0 %attend_blocks.1 = bf16[8,8,512]{2,1,0:T(8,128)(2,1)} custom-call(s32[8]{0:T(128)} %ctx_ref.1, f32[8,8,640]{2,1,0:T(8,128)} %maximum_maximum_fusion.q_ref, f32[8,1,512]{2,1,0:T(1,128)} %reshape.116.cn_ref, f32[8,1,64]{2,1,0:T(1,128)} %maximum_convert_fusion.1.kn_ref, bf16[8,2048,512]{2,1,0:T(8,128)(2,1)} %c_hbm.1, bf16[8,64,2048]{2,1,0:T(8,128)(2,1)} %bitcast.15), custom_call_target="tpu_custom_call" | custom-call | tf_op jit(solution)/shard_map/attend_blocks/pallas_call | solution.py:279
  92.8 6.3 %fusion.part_ref = f32[8,5120]{1,0:T(8,128)} fusion(bf16[16384,5120]{1,0:T(8,128)(2,1)} %param.20, s32[]{:T(128)S(6)} %select_n.12, bf16[512,8,128]{2,1,0:T(8,128)(2,1)S(1)} %get-tuple-element.12, bf16[8,8,512]{2,1,0:T(8,128)(2,1)} %attend_blocks.1), kind=kOutput, calls=%fused_computation | convolution fusion | flops 92282880 | bytes 11763716 | tf_op jit(solution)/shard_map/dot_general | solution.py:395
  99.1 21.3 %add_up.1 = bf16[8,5120]{1,0:T(8,128)(2,1)} custom-call(f32[8,5120]{1,0:T(8,128)} %fusion.part_ref, bf16[8,5120]{1,0:T(8,128)(2,1)} %x_ref.1), custom_call_target="tpu_custom_call" | custom-call | tf_op jit(solution)/shard_map/add_up/pallas_call | solution.py:359
  120.4 0.7 pad_maximum_fusion
  121.1 1.5 %copy.45 = bf16[8,5120]{1,0:T(8,128)(2,1)} copy(bf16[8,5120]{1,0:T(8,128)(2,1)} %add_up.1) | data formatting | bytes 163840
  122.6 0.0 copy-done.1
  (10 shorter events, 0.1 us)
Async XLA Ops:
  0.6 9.6 %copy-start.2 = (f32[1536]{0:T(1024)S(1)}, f32[1536]{0:T(1024)}, u32[]{:S(2)}) copy-start(f32[1536]{0:T(1024)} %param.14) | copy-start | bytes 18436
  0.6 12.8 %copy-start = (bf16[8,5120]{1,0:T(8,128)(2,1)S(1)}, bf16[8,5120]{1,0:T(8,128)(2,1)}, u32[]{:S(2)}) copy-start(bf16[8,5120]{1,0:T(8,128)(2,1)} %x_ref.1) | copy-start | bytes 245764
  2.4 15.4 %copy-start.4 = (s32[8]{0:T(128)S(1)}, s32[8]{0:T(128)}, u32[]{:S(2)}) copy-start(s32[8]{0:T(128)} %ctx_ref.1) | copy-start | bytes 100
  2.4 17.0 %copy-start.3 = (f32[512]{0:T(512)S(1)}, f32[512]{0:T(512)}, u32[]{:S(2)}) copy-start(f32[512]{0:T(512)} %param.17) | copy-start | bytes 6148
  19.5 103.2 %copy-start.1 = (bf16[8,512]{1,0:T(8,128)(2,1)}, bf16[8,512]{1,0:T(8,128)(2,1)S(1)}, u32[]{:S(2)}) copy-start(bf16[8,512]{1,0:T(8,128)(2,1)S(1)} %multiply_convert_fusion.2) | copy-start | bytes 24580

commit v2 on v0

v2 whole, which is shorter than its diff:
```python
import functools

import jax
import jax.numpy as jnp
from jax import lax
from jax.experimental import pallas as pl
from jax.experimental.pallas import tpu as pltpu
from jax.sharding import PartitionSpec as P

NORM_EPS = 1e-6
ROPE_THETA = 10000.0
LANES = 128
RELAY_TURN = 2
FAR_TURN = 4
LOWEST = float(jnp.finfo(jnp.float32).min)
MESH = pl.DeviceIdType.MESH


def rms_norm(values, gain_vec):
    mean_sq = jnp.mean(jnp.square(values), axis=-1, keepdims=True)
    return values * lax.rsqrt(mean_sq + NORM_EPS) * gain_vec


def rope_tables(positions, rope_dim):
    half_dim = rope_dim // 2
    inv_freq = ROPE_THETA ** (-2.0 * jnp.arange(half_dim, dtype=jnp.float32) / rope_dim)
    angles = positions.astype(jnp.float32)[..., None] * inv_freq
    return jnp.cos(angles), jnp.sin(angles)


def rope_rotate(values, cos_tab, sin_tab):
    half_dim = values.shape[-1] // 2
    swapped = jnp.concatenate([values[:, half_dim:], values[:, :half_dim]], axis=-1)
    return values * cos_tab + swapped * sin_tab


def merge(blocks, latent):
    half = LANES // 2
    tops = [block[:, latent:latent + 1] for block in blocks]
    top = functools.reduce(jnp.maximum, tops)
    factors = [jnp.exp(one - top) for one in tops]
    acc = sum(block[:, :latent] * factor for block, factor in zip(blocks, factors))
    mass = sum(block[:, latent + half:latent + half + 1] * factor for block, factor in zip(blocks, factors))
    return acc, top, mass


def put_block(ref, index, acc, top, mass):
    latent = acc.shape[-1]
    rows = acc.shape[0]
    shape = ref.at[index].shape
    half = LANES // 2
    ref[index + (slice(None),) * (len(shape) - 1) + (slice(0, latent),)] = acc.reshape(shape[:-1] + (latent,))
    stats = jnp.where(lax.broadcasted_iota(jnp.int32, (rows, LANES), 1) < half, top, mass)
    ref[index + (slice(None),) * (len(shape) - 1) + (slice(latent, latent + LANES),)] = stats.reshape(shape[:-1] + (LANES,))


def decode_kernel(nz, scale, ctx_ref, x_ref, gq_ref, gkv_ref, cos_ref, sin_ref,
                  wdq_hbm, wuq_hbm, wdkv_hbm, wuk_hbm, wuv_hbm, wo_hbm, c_hbm, k_hbm, out_ref, cnew_ref, knew_ref,
                  c_buf, k_buf, q_all, s_buf, own, other, mine, held, relay, last,
                  big, wuq_buf, wdkv_buf, uk_buf, uv_buf, wide, uk_heads, uv_heads,
                  cq_half, q_ref, cn_ref, kn_ref, o_lat, part, got, pair,
                  c_sem, k_sem, q_recv, q_send, q_send_x, x_send, x_recv, h_send, h_recv, f_send, f_recv,
                  w_sem, s_sem, r_sem, a_send, a_recv, b_send, b_recv):
    n_req, t_dev, latent = c_buf.shape
    rope_dim = k_buf.shape[1]
    per = q_ref.shape[1]
    q_half = cq_half.shape[2]
    v_dim = uv_heads.shape[2]
    nope_dim = uk_heads.shape[2]
    width = part.shape[2]
    n_dev = 2 * nz
    heads = n_dev * per
    me = lax.axis_index('cp')
    z, core = me // 2, me % 2
    partner = me + 1 - 2 * core
    at = lambda off: lax.rem(z + off + nz, nz)
    chip = lambda off: at(off) * 2 + core

    def remote(src, dst, send, recv, target):
        return pltpu.make_async_remote_copy(src_ref=src, dst_ref=dst, send_sem=send, recv_sem=recv,
                                            device_id={'cp': target}, device_id_type=MESH)

    rows = big.shape[0]
    head0 = pl.multiple_of(me * per, 8)
    weights = [pltpu.make_async_copy(wuk_hbm.at[:, pl.ds(head0, per)], uk_buf, w_sem.at[0])]
    q_cols = pl.ds(pl.multiple_of(core * q_half, LANES), q_half)
    blocks = x_ref.shape[1] // rows
    for i in range(blocks):
        weights.append(pltpu.make_async_copy(wdq_hbm.at[i * rows:(i + 1) * rows, q_cols], big.at[:, i * q_half:(i + 1) * q_half], w_sem.at[4 + i]))
    uq_cols = wuq_buf.shape[1]
    weights.append(pltpu.make_async_copy(wuq_hbm.at[:, pl.ds(pl.multiple_of(me * uq_cols, LANES), uq_cols)], wuq_buf, w_sem.at[1]))
    weights.append(pltpu.make_async_copy(wdkv_hbm, wdkv_buf, w_sem.at[2]))
    weights.append(pltpu.make_async_copy(wuv_hbm.at[:, pl.ds(head0, per)], uv_buf, w_sem.at[3]))
    for copy in weights:
        copy.start()
    for r in range(n_req):
        pltpu.make_async_copy(c_hbm.at[r], c_buf.at[r], c_sem.at[r]).start()
        pltpu.make_async_copy(k_hbm.at[r], k_buf.at[r], k_sem.at[r]).start()
    wait_uk, *wait_dq, wait_uq, wait_dkv, wait_uv = weights
    wo_copy = pltpu.make_async_copy(wo_hbm.at[pl.ds(pl.multiple_of(me * rows, LANES), rows)], big, w_sem.at[4])

    barrier = pltpu.get_barrier_semaphore()
    for peer in (*(chip(off) for off in range(1, nz)), partner):
        pl.semaphore_signal(barrier, inc=1, device_id={'cp': peer}, device_id_type=MESH)

    def by_head(src, dst):
        step = 64

        def widen(i, carry):
            wide[pl.ds(i * step, step)] = src[pl.ds(i * step, step)].astype(jnp.float32)
            return carry
        lax.fori_loop(0, latent // step, widen, 0)
        for h in range(per):
            dst[h] = wide[:, h, :].astype(jnp.bfloat16)

    wait_uk.wait()
    by_head(uk_buf, uk_heads)
    x = x_ref[...]
    cq = jnp.zeros((n_req, q_half), jnp.float32)
    for i in range(blocks):
        wait_dq[i].wait()
        cq += jnp.dot(x[:, i * rows:(i + 1) * rows], big[:, i * q_half:(i + 1) * q_half], preferred_element_type=jnp.float32)
    cq_half[core] = cq.astype(jnp.bfloat16).astype(jnp.float32)
    wo_copy.start()
    pl.semaphore_wait(barrier, nz)
    cq_copy = remote(cq_half.at[core], cq_half.at[core], s_sem.at[0], r_sem.at[0], partner)
    cq_copy.start()
    cq_copy.wait_recv()
    cq = jnp.concatenate([cq_half[0], cq_half[1]], axis=1)
    cq_norm = rms_norm(cq, gq_ref[...]).astype(jnp.bfloat16)
    wait_uq.wait()
    q_full = jnp.dot(cq_norm, wuq_buf[...], preferred_element_type=jnp.float32).astype(jnp.bfloat16)
    for h in range(per):
        q_h = q_full[:, h * (nope_dim + rope_dim):(h + 1) * (nope_dim + rope_dim)]
        q_lat = lax.dot_general(q_h[:, :nope_dim], uk_heads[h], (((1,), (1,)), ((), ())), preferred_element_type=jnp.float32)
        q_rope = rope_rotate(q_h[:, nope_dim:].astype(jnp.float32), cos_ref[...], sin_ref[...])
        q_ref[:, h, :latent] = q_lat.astype(jnp.bfloat16).astype(jnp.float32)
        q_rope = jnp.concatenate([q_rope, jnp.zeros((n_req, LANES - rope_dim), jnp.float32)], axis=1)
        q_ref[:, h, latent:] = q_rope.astype(jnp.bfloat16).astype(jnp.float32)
    q_all[:, pl.ds(me, 1)] = q_ref[...].reshape(n_req, 1, per, latent + LANES)

    def new_entry():
        wait_dkv.wait()
        kv = lax.dot_general(x_ref[...], wdkv_buf[...], (((1,), (1,)), ((), ())), preferred_element_type=jnp.float32)
        c_new = rms_norm(kv[:, :latent], gkv_ref[...]).astype(jnp.bfloat16)
        kr_new = rope_rotate(kv[:, latent:], cos_ref[...], sin_ref[...]).astype(jnp.bfloat16)
        cnew_ref[...] = c_new
        knew_ref[...] = kr_new
        cn_ref[...] = c_new.astype(jnp.float32)
        kn_ref[...] = kr_new.astype(jnp.float32)
        wait_uv.wait()
        by_head(uv_buf, uv_heads)

    def q_copy(r, sem, src_dev, off):
        src = q_ref.at[r] if sem < 4 else q_all.at[r, src_dev]
        return remote(src, q_all.at[r, src_dev], q_send.at[r, sem], q_recv.at[r, src_dev], chip(off))

    def cross_copy(r, slot, src_dev):
        src = q_ref.at[r] if slot == 0 else q_all.at[r, src_dev]
        return remote(src, q_all.at[r, src_dev], q_send_x.at[r, slot], q_recv.at[r, src_dev], partner)

    def arrived(r, src_dev):
        remote(q_all.at[r, src_dev], q_all.at[r, src_dev], q_send.at[r, 0], q_recv.at[r, src_dev], partner).wait_recv()

    def gather_near(r):
        for sem, off in enumerate((2, -2, 1, -1)):
            q_copy(r, sem, me, off).start()
        cross_copy(r, 0, me).start()

    def gather_relay(r):
        for way, side in enumerate((1, -1)):
            src_dev = chip(-2 * side)
            arrived(r, src_dev)

            @pl.when(core == way)
            def _(side=side, src_dev=src_dev):
                q_copy(r, 6, src_dev, 2 * side).start()
            q_copy(r, 4 + way, src_dev, side).start()
            cross_copy(r, 1 + way, src_dev).start()
        for way, side in enumerate((1, -1)):
            arrived(r, chip(side))
            cross_copy(r, 3 + way, chip(side)).start()

    def gather_far(r):
        for slot, off in ((5, 3), (6, -3), (7, 4)):
            arrived(r, chip(off))
            cross_copy(r, slot, chip(off)).start()

    def attend(r):
        def from_partner(d, carry):
            arrived(r, d * 2 + 1 - core)
            return carry
        lax.fori_loop(0, nz, from_partner, 0)
        pltpu.make_async_copy(c_hbm.at[r], c_buf.at[r], c_sem.at[r]).wait()
        pltpu.make_async_copy(k_hbm.at[r], k_buf.at[r], k_sem.at[r]).wait()
        q = q_all[r].reshape(heads, latent + LANES)
        q_lat = q[:, :latent].astype(jnp.bfloat16)
        q_rope = q[:, latent:latent + rope_dim].astype(jnp.bfloat16)
        n = ctx_ref[r]
        base = me * t_dev
        step = 512
        top = jnp.full((heads, LANES), LOWEST, jnp.float32)

        def valid(t0):
            return base + t0 + lax.broadcasted_iota(jnp.int32, (1, step), 1) < n

        for t0 in range(0, t_dev, step):
            s = lax.dot_general(q_lat, c_buf[r, t0:t0 + step, :], (((1,), (1,)), ((), ())), preferred_element_type=jnp.float32)
            s += jnp.dot(q_rope, k_buf[r, :, t0:t0 + step], preferred_element_type=jnp.float32)
            s = jnp.where(valid(t0), s * scale, LOWEST)
            s_buf[:, t0:t0 + step] = s
            for j in range(0, step, LANES):
                top = jnp.maximum(top, s[:, j:j + LANES])
        c_new = cn_ref[pl.ds(r, 1)]
        kr_new = kn_ref[pl.ds(r, 1)]
        s_new = (jnp.sum(q_lat.astype(jnp.float32) * c_new, axis=1, keepdims=True)
                 + jnp.sum(q_rope.astype(jnp.float32) * kr_new, axis=1, keepdims=True)) * scale
        owner = jnp.logical_and(n >= base, n < base + t_dev)
        s_new = jnp.where(owner, s_new, LOWEST)
        m = jnp.maximum(jnp.max(top, axis=1, keepdims=True), s_new)
        w_new = jnp.where(owner, jnp.exp(s_new - m), 0.0)
        mass = jnp.zeros((heads, LANES), jnp.float32)
        acc = w_new.astype(jnp.bfloat16).astype(jnp.float32) * c_new
        for t0 in range(0, t_dev, step):
            w = jnp.where(valid(t0), jnp.exp(s_buf[:, t0:t0 + step] - m), 0.0)
            for j in range(0, step, LANES):
                mass += w[:, j:j + LANES]
            acc += jnp.dot(w.astype(jnp.bfloat16), c_buf[r, t0:t0 + step, :], preferred_element_type=jnp.float32)
        put_block(own, (r,), acc, m, jnp.sum(mass, axis=1, keepdims=True) + w_new)

    def cross_sum(r):
        return remote(own.at[r, :, 1 - core], other.at[r], x_send.at[r], x_recv.at[r], partner)

    def flat(block):
        return block.reshape(-1, latent + LANES)

    def hold_copy(r, sem):
        dest, side, slot, off = ((3, 1, 0, 1), (-3, 0, 0, -1), (-1, 0, 1, 1), (1, 1, 1, -1))[sem]
        return remote(mine.at[r, at(dest)], held.at[r, side, slot], h_send.at[r, sem], h_recv.at[r, side, slot], chip(off))

    def far_copy(r, side):
        return remote(mine.at[r, at(4)], held.at[r, side, 2], h_send.at[r, 4], h_recv.at[r, side, 2], chip(4 * side - 2))

    def relay_copy(r, side):
        return remote(relay.at[r, side], last.at[r, side], f_send.at[r, side], f_recv.at[r, side], chip(4 * side - 2))

    def reduce_pair(r):
        cross_sum(r).wait_recv()
        put_block(mine, (r,), *merge([flat(own[r, :, core]), flat(other[r])], latent))
        for side in range(2):
            @pl.when(core == side)
            def _(side=side):
                far_copy(r, side).start()
        for sem in range(4):
            hold_copy(r, sem).start()

    def reduce_relay(r):
        for side in range(2):
            for slot in range(2):
                remote(mine.at[r, 0], held.at[r, side, slot], h_send.at[r, 0], h_recv.at[r, side, slot], partner).wait_recv()

            @pl.when(core == side)
            def _(side=side):
                far_copy(r, side).wait_recv()
        got = [jnp.concatenate([held[r, 0, slot], held[r, 1, slot]]) for slot in range(3)]
        put_block(relay, (r,), *merge([jnp.concatenate([mine[r, at(-2)], mine[r, at(2)]]), *got], latent))
        for side in range(2):
            relay_copy(r, side).start()

    def finish(r):
        for side in range(2):
            relay_copy(r, side).wait_recv()
        acc, _, mass = merge([mine[r, z], last[r, 0], last[r, 1]], latent)
        o_lat[r] = acc / mass

    lane = lax.broadcasted_iota(jnp.int32, (n_req, per, latent + LANES), 2)
    empty = jnp.where(jnp.logical_and(lane >= latent, lane < latent + LANES // 2), LOWEST, 0.0)
    for side in range(2):
        @pl.when(core != side)
        def _(side=side):
            held[:, side, 2] = empty

    def slot(s, carry):
        def at_slot(delay, body):
            r = s - delay

            @pl.when(jnp.logical_and(r >= 0, r < n_req))
            def _():
                body(r)

        at_slot(FAR_TURN, gather_far)
        at_slot(RELAY_TURN, gather_relay)
        at_slot(turn + 6, finish)
        at_slot(turn + 4, reduce_relay)
        at_slot(turn + 2, reduce_pair)

        def compute(r):
            attend(r)
            cross_sum(r).start()
        at_slot(turn, compute)
        return carry

    def near(r, carry):
        gather_near(r)
        return carry
    lax.fori_loop(0, n_req, near, 0)
    new_entry()
    turn = FAR_TURN + 1
    lax.fori_loop(0, n_req + turn + 6, slot, 0)

    o_heads = []
    for h in range(per):
        o_heads.append(jnp.dot(o_lat[:, h, :].astype(jnp.bfloat16), uv_heads[h], preferred_element_type=jnp.float32).astype(jnp.bfloat16))
    o_heads = jnp.concatenate(o_heads, axis=1)
    wo_copy.wait()
    order = sorted(range(1, nz), key=lambda off: -min(off, nz - off)) + [0]

    def piece_copy(off):
        return remote(part.at[at(off)], got.at[off - 1], a_send.at[off - 1], a_recv.at[off - 1], chip(off))

    for off in order:
        cols = pl.ds(pl.multiple_of(at(off) * width, LANES), width)
        part[at(off)] = jnp.dot(o_heads, big[:, cols], preferred_element_type=jnp.float32)
        if off:
            piece_copy(off).start()
    acc = part[z]
    for off in order[-2::-1]:
        piece_copy(off).wait_recv()
        acc += got[off - 1]
    pair[core] = acc
    swap = remote(pair.at[core], pair.at[core], s_sem.at[1], r_sem.at[1], partner)
    swap.start()
    swap.wait_recv()
    part_cols = lambda piece: pl.ds(pl.multiple_of(piece * width, LANES), width)
    got_all = got.at[nz - 1]
    got_all[...] = pair[0] + pair[1]
    out_ref[:, part_cols(z)] = got_all[...]

    def spread(off):
        return remote(got_all, out_ref.at[:, part_cols(z)], b_send.at[off - 1], b_recv.at[off - 1], chip(off))
    for off in order[:-1]:
        spread(off).start()
    for off in order[-2::-1]:
        spread(off).wait_recv()
    cq_copy.wait_send()
    swap.wait_send()
    for off in order[:-1]:
        piece_copy(off).wait_send()
        spread(off).wait_send()

    def drain(r, carry):
        for sem in range(7):
            q_copy(r, sem, me, 1).wait_send()
        for slot_x in range(nz):
            cross_copy(r, slot_x, me).wait_send()
        cross_sum(r).wait_send()
        for sem in range(4):
            hold_copy(r, sem).wait_send()
        far_copy(r, 0).wait_send()
        for side in range(2):
            relay_copy(r, side).wait_send()
        return carry
    lax.fori_loop(0, n_req, drain, 0)


def decode_group(nz, ctx_len, x, g_q, g_kv, cos_tab, sin_tab, w_dq, w_uq, w_dkv_t, w_uk, w_uv, w_o, cache_c, cache_krt, scale):
    n_req, d_model = x.shape
    _, t_dev, latent = cache_c.shape
    rope_dim = cache_krt.shape[1]
    n_dev = 2 * nz
    _, heads, nope_dim = w_uk.shape
    v_dim = w_uv.shape[2]
    per = heads // n_dev
    width = latent + LANES
    q_lora = w_dq.shape[1]
    rows = per * v_dim
    vmem = pl.BlockSpec(memory_space=pltpu.VMEM)
    hbm = pl.BlockSpec(memory_space=pl.ANY)
    dma = pltpu.SemaphoreType.DMA
    f32, bf16 = jnp.float32, jnp.bfloat16
    return pl.pallas_call(
        functools.partial(decode_kernel, nz, scale),
        out_shape=(jax.ShapeDtypeStruct((n_req, d_model), f32),
                   jax.ShapeDtypeStruct((n_req, latent), bf16),
                   jax.ShapeDtypeStruct((n_req, rope_dim), bf16)),
        in_specs=[pl.BlockSpec(memory_space=pltpu.SMEM)] + [vmem] * 5 + [hbm] * 8,
        out_specs=(vmem, vmem, vmem),
        scratch_shapes=[
            pltpu.VMEM((n_req, t_dev, latent), bf16),
            pltpu.VMEM((n_req, rope_dim, t_dev), bf16),
            pltpu.VMEM((n_req, n_dev, per, width), f32),
            pltpu.VMEM((heads, t_dev), f32),
            pltpu.VMEM((n_req, nz, 2, per, width), f32),
            pltpu.VMEM((n_req, nz, per, width), f32),
            pltpu.VMEM((n_req, nz, per, width), f32),
            pltpu.VMEM((n_req, 2, 3, per, width), f32),
            pltpu.VMEM((n_req, 2, per, width), f32),
            pltpu.VMEM((n_req, 2, per, width), f32),
            pltpu.VMEM((rows, d_model), bf16),
            pltpu.VMEM((q_lora, per * (nope_dim + rope_dim)), bf16),
            pltpu.VMEM((latent + rope_dim, d_model), bf16),
            pltpu.VMEM((latent, per, nope_dim), bf16),
            pltpu.VMEM((latent, per, v_dim), bf16),
            pltpu.VMEM((latent, per, v_dim), f32),
            pltpu.VMEM((per, latent, nope_dim), bf16),
            pltpu.VMEM((per, latent, v_dim), bf16),
            pltpu.VMEM((2, n_req, q_lora // 2), f32),
            pltpu.VMEM((n_req, per, width), f32),
            pltpu.VMEM((n_req, latent), f32),
            pltpu.VMEM((n_req, rope_dim), f32),
            pltpu.VMEM((n_req, per, latent), f32),
            pltpu.VMEM((nz, n_req, d_model // nz), f32),
            pltpu.VMEM((nz, n_req, d_model // nz), f32),
            pltpu.VMEM((2, n_req, d_model // nz), f32),
            dma((n_req,)),
            dma((n_req,)),
            dma((n_req, n_dev)),
            dma((n_req, 7)),
            dma((n_req, nz)),
            dma((n_req,)),
            dma((n_req,)),
            dma((n_req, 5)),
            dma((n_req, 2, 3)),
            dma((n_req, 2)),
            dma((n_req, 2)),
            dma((4 + d_model // rows,)),
            dma((2,)), dma((2,)),
            dma((nz - 1,)), dma((nz - 1,)), dma((nz - 1,)), dma((nz - 1,)),
        ],
        compiler_params=pltpu.CompilerParams(collective_id=0, has_side_effects=True, vmem_limit_bytes=67_000_000),
        name='decode_group',
    )(ctx_len, x, g_q.reshape(1, -1), g_kv.reshape(1, -1), cos_tab, sin_tab, w_dq, w_uq, w_dkv_t, w_uk, w_uv, w_o, cache_c, cache_krt)


def solution(mesh):
    nz = mesh.shape['cp'] // 2

    def decode_step(x, w_dq, g_q, w_uq, w_dkv, g_kv, w_uk, w_uv, w_o, cache_c, cache_kr, ctx_len):
        rope_dim = cache_kr.shape[2]
        scale = (w_uk.shape[2] + rope_dim) ** -0.5
        cos_tab, sin_tab = rope_tables(ctx_len, rope_dim)
        cos_tab = jnp.concatenate([cos_tab, cos_tab], axis=1)
        sin_tab = jnp.concatenate([-sin_tab, sin_tab], axis=1)
        attn_out, c_new, kr_new = decode_group(nz, ctx_len, x, g_q, g_kv, cos_tab, sin_tab, w_dq, w_uq, w_dkv.T, w_uk, w_uv, w_o,
                                               cache_c, cache_kr.transpose(0, 2, 1), scale)
        return (x.astype(jnp.float32) + attn_out).astype(jnp.bfloat16), c_new, kr_new

    spec_rows = P('dp', None)
    spec_cache = P('dp', 'cp', None)
    in_specs = (spec_rows, P(), P(), P(), P(), P(), P(), P(), P(), spec_cache, spec_cache, P('dp'))
    out_specs = (spec_rows, spec_rows, spec_rows)
    return jax.shard_map(decode_step, mesh=mesh, in_specs=in_specs, out_specs=out_specs, check_vma=False)
```

time: 409 us -> 90 us (0.22); the launches traced: 404 us -> 89.7 us
  waiting for transfers between devices: 183 us -> 0 us
  matrix products: 170 us -> 0 us
  Pallas kernels: 0 us -> 82.2 us
  other arithmetic: 26.6 us -> 3.07 us
  between operations: 14.5 us -> 0.64 us
  local copies, waits for them, and re-layouts: 9.79 us -> 3.84 us
    all_gather x1 -> x0, waiting for transfers between devices: 183 us -> none  [decode_step(): gathered = lax.all_gather(packed, 'cp')]
    dot_general x10 -> x0, matrix products: 170 us -> none  [the longest x1 59.7 us: output_step(): jnp.dot(o_heads.reshape(x.shape[0], -1), w_o, preferred_element_type=jnp....]
    pallas_call x0 -> x1, Pallas kernels: none -> 82.2 us  [decode_group(): pl.pallas_call(functools.partial(decode_kernel, nz, scale), out_shape=(ja...]
    reduce_sum x4 -> x0, other arithmetic: 16.3 us -> none  [the longest x1 13.4 us: decode_step(): lat_sum = jnp.sum(factor[:, :, :, None] * gathered[:, :, :, 2:], axis=0)]
  transfers between devices with their start and end apart: 1 -> 0, of which waited for: 1 -> 0; matrix products, arithmetic and copies ran while one was open for 0% -> 0% of each run, Pallas kernels for 0% -> 0%
where the time goes in v2:
time: 90 us; the launch traced here: 89.7 us
  Pallas kernels  82.2 us (91%)
  local copies, waits for them, and re-layouts  3.84 us (4%)
  other arithmetic  3.07 us (3%)
    pallas_call x1, Pallas kernels, decode_group(): pl.pallas_call(functools.partial(decode_kernel, nz, scale), out_shape=(ja...  82.2 us
    unnamed x2, local copies, waits for them, and re-layouts  2.54 us

profile of v2, /device:TPU:21, one launch (start us, length us, event | category | flops | bytes accessed | tf_op | source)
XLA Modules:
  0.0 89.7 jit_solution(343567867555500571)
XLA Ops:
  0.6 0.7 convert_element_type.10
  1.3 1.3 %reshape.18.gq_ref = f32[1,1536]{1,0:T(1,128)} reshape(f32[1536]{0:T(1024)} %param.14) | data formatting | bytes 12288 | tf_op jit(solution)/shard_map/reshape | solution.py:432
  2.6 0.1 fusion
  2.7 0.7 pad_maximum_fusion
  3.4 82.2 %decode_group.1 = (f32[8,5120]{1,0:T(8,128)}, bf16[8,512]{1,0:T(8,128)(2,1)}, bf16[8,64]{1,0:T(8,128)(2,1)}) custom-call(s32[8]{0:T(128)} %ctx_ref.1, bf16[8,5120]{1,0:T(8,128)(2,1)} %x_ref.1, f32[1,1536]{1,0:T(1,128)} %reshape.18.gq_ref, f32[1,512]{1,0:T(1,128)} %bitcast.5, f32[8,64]{1,0:T(8,128)} %get-tuple-element.12.cos_ref, ...), custom_call_target="tpu_custom_call" | custom-call | tf_op jit(solution)/shard_map/decode_group/pallas_call | solution.py:381
  85.6 1.6 %add_convert_fusion = bf16[8,5120]{1,0:T(8,128)(2,1)} fusion(f32[8,5120]{1,0:T(8,128)} %get-tuple-element.6, bf16[8,5120]{1,0:T(8,128)(2,1)} %x_ref.1), kind=kLoop, calls=%fused_computation | loop fusion | flops 122880 | bytes 327680 | tf_op jit(solution)/shard_map/convert_element_type | solution.py:446
  87.2 1.3 %copy.17 = bf16[8,512]{1,0:T(8,128)(2,1)} copy(bf16[8,512]{1,0:T(8,128)(2,1)} %get-tuple-element.18) | data formatting | bytes 16384
  88.5 1.2 %copy.18 = bf16[8,64]{1,0:T(8,128)(2,1)} copy(bf16[8,64]{1,0:T(8,128)(2,1)} %get-tuple-element.19) | data formatting | bytes 2048
  (1 shorter events, 0.0 us)

commit v3 on v2

--- a/solution.py
+++ b/solution.py
@@ -10,6 +10,8 @@
 NORM_EPS = 1e-6
 ROPE_THETA = 10000.0
 LANES = 128
+AHEAD = 3
+RS_TURN = 3
 RELAY_TURN = 2
 FAR_TURN = 4
 LOWEST = float(jnp.finfo(jnp.float32).min)
@@ -23,9 +25,11 @@
 
 def rope_tables(positions, rope_dim):
     half_dim = rope_dim // 2
-    inv_freq = ROPE_THETA ** (-2.0 * jnp.arange(half_dim, dtype=jnp.float32) / rope_dim)
+    lane = jnp.arange(rope_dim)
+    inv_freq = ROPE_THETA ** (-2.0 * (lane % half_dim).astype(jnp.float32) / rope_dim)
     angles = positions.astype(jnp.float32)[..., None] * inv_freq
-    return jnp.cos(angles), jnp.sin(angles)
+    sines = jnp.sin(angles)
+    return jnp.cos(angles), jnp.where(lane < half_dim, -sines, sines)
 
 
 def rope_rotate(values, cos_tab, sin_tab):
@@ -58,12 +62,13 @@
                   wdq_hbm, wuq_hbm, wdkv_hbm, wuk_hbm, wuv_hbm, wo_hbm, c_hbm, k_hbm, out_ref, cnew_ref, knew_ref,
                   c_buf, k_buf, q_all, s_buf, own, other, mine, held, relay, last,
                   big, wuq_buf, wdkv_buf, uk_buf, uv_buf, wide, uk_heads, uv_heads,
-                  cq_half, q_ref, cn_ref, kn_ref, o_lat, part, got, pair,
+                  cq_half, q_ref, rope_ref, cn_ref, kn_ref, o_lat, part, got, pair,
                   c_sem, k_sem, q_recv, q_send, q_send_x, x_send, x_recv, h_send, h_recv, f_send, f_recv,
                   w_sem, s_sem, r_sem, a_send, a_recv, b_send, b_recv):
     n_req, t_dev, latent = c_buf.shape
     rope_dim = k_buf.shape[1]
     per = q_ref.shape[1]
+    wide_row = latent + LANES
     q_half = cq_half.shape[2]
     v_dim = uv_heads.shape[2]
     nope_dim = uk_heads.shape[2]
@@ -91,12 +96,9 @@
     weights.append(pltpu.make_async_copy(wuq_hbm.at[:, pl.ds(pl.multiple_of(me * uq_cols, LANES), uq_cols)], wuq_buf, w_sem.at[1]))
     weights.append(pltpu.make_async_copy(wdkv_hbm, wdkv_buf, w_sem.at[2]))
     weights.append(pltpu.make_async_copy(wuv_hbm.at[:, pl.ds(head0, per)], uv_buf, w_sem.at[3]))
-    for copy in weights:
+    wait_uk, *wait_dq, wait_uq, wait_dkv, wait_uv = weights
+    for copy in weights[:-2]:
         copy.start()
-    for r in range(n_req):
-        pltpu.make_async_copy(c_hbm.at[r], c_buf.at[r], c_sem.at[r]).start()
-        pltpu.make_async_copy(k_hbm.at[r], k_buf.at[r], k_sem.at[r]).start()
-    wait_uk, *wait_dq, wait_uq, wait_dkv, wait_uv = weights
     wo_copy = pltpu.make_async_copy(wo_hbm.at[pl.ds(pl.multiple_of(me * rows, LANES), rows)], big, w_sem.at[4])
 
     barrier = pltpu.get_barrier_semaphore()
@@ -121,38 +123,44 @@
         wait_dq[i].wait()
         cq += jnp.dot(x[:, i * rows:(i + 1) * rows], big[:, i * q_half:(i + 1) * q_half], preferred_element_type=jnp.float32)
     cq_half[core] = cq.astype(jnp.bfloat16).astype(jnp.float32)
-    wo_copy.start()
     pl.semaphore_wait(barrier, nz)
     cq_copy = remote(cq_half.at[core], cq_half.at[core], s_sem.at[0], r_sem.at[0], partner)
     cq_copy.start()
     cq_copy.wait_recv()
     cq = jnp.concatenate([cq_half[0], cq_half[1]], axis=1)
-    cq_norm = rms_norm(cq, gq_ref[...]).astype(jnp.bfloat16)
+    cq_norm = rms_norm(cq, gq_ref[...][None]).astype(jnp.bfloat16)
     wait_uq.wait()
+    wait_dkv.start()
+    for r in range(n_req):
+        pltpu.make_async_copy(c_hbm.at[r], c_buf.at[r], c_sem.at[r]).start()
+        pltpu.make_async_copy(k_hbm.at[r], k_buf.at[r], k_sem.at[r]).start()
+    wait_uv.start()
+    wo_copy.start()
     q_full = jnp.dot(cq_norm, wuq_buf[...], preferred_element_type=jnp.float32).astype(jnp.bfloat16)
     for h in range(per):
         q_h = q_full[:, h * (nope_dim + rope_dim):(h + 1) * (nope_dim + rope_dim)]
         q_lat = lax.dot_general(q_h[:, :nope_dim], uk_heads[h], (((1,), (1,)), ((), ())), preferred_element_type=jnp.float32)
         q_rope = rope_rotate(q_h[:, nope_dim:].astype(jnp.float32), cos_ref[...], sin_ref[...])
-        q_ref[:, h, :latent] = q_lat.astype(jnp.bfloat16).astype(jnp.float32)
+        q_ref[1:, h, :] = q_lat.astype(jnp.bfloat16).astype(jnp.float32)
         q_rope = jnp.concatenate([q_rope, jnp.zeros((n_req, LANES - rope_dim), jnp.float32)], axis=1)
-        q_ref[:, h, latent:] = q_rope.astype(jnp.bfloat16).astype(jnp.float32)
-    q_all[:, pl.ds(me, 1)] = q_ref[...].reshape(n_req, 1, per, latent + LANES)
+        rope_ref[:, h, :] = q_rope.astype(jnp.bfloat16).astype(jnp.float32)
+    for r in range(0, n_req, 2):
+        both = jnp.concatenate([rope_ref[r, :, :rope_dim], rope_ref[r + 1, :, :rope_dim]], axis=1)
+        q_ref[0, :, r * rope_dim:(r + 2) * rope_dim] = both
+    q_all[:, pl.ds(me, 1)] = q_ref[...].reshape(n_req + 1, 1, per, latent)
 
     def new_entry():
         wait_dkv.wait()
         kv = lax.dot_general(x_ref[...], wdkv_buf[...], (((1,), (1,)), ((), ())), preferred_element_type=jnp.float32)
-        c_new = rms_norm(kv[:, :latent], gkv_ref[...]).astype(jnp.bfloat16)
+        c_new = rms_norm(kv[:, :latent], gkv_ref[...][None]).astype(jnp.bfloat16)
         kr_new = rope_rotate(kv[:, latent:], cos_ref[...], sin_ref[...]).astype(jnp.bfloat16)
         cnew_ref[...] = c_new
         knew_ref[...] = kr_new
         cn_ref[...] = c_new.astype(jnp.float32)
         kn_ref[...] = kr_new.astype(jnp.float32)
-        wait_uv.wait()
-        by_head(uv_buf, uv_heads)
 
     def q_copy(r, sem, src_dev, off):
-        src = q_ref.at[r] if sem < 4 else q_all.at[r, src_dev]
+        src = q_ref.at[r] if src_dev is me else q_all.at[r, src_dev]
         return remote(src, q_all.at[r, src_dev], q_send.at[r, sem], q_recv.at[r, src_dev], chip(off))
 
     def cross_copy(r, slot, src_dev):
@@ -162,40 +170,60 @@
     def arrived(r, src_dev):
         remote(q_all.at[r, src_dev], q_all.at[r, src_dev], q_send.at[r, 0], q_recv.at[r, src_dev], partner).wait_recv()
 
-    def gather_near(r):
+    def gather_near(i, carry):
         for sem, off in enumerate((2, -2, 1, -1)):
-            q_copy(r, sem, me, off).start()
-        cross_copy(r, 0, me).start()
-
-    def gather_relay(r):
+            q_copy(i, sem, me, off).start()
+        cross_copy(i, 0, me).start()
+        return carry
+
+    def gather_later(r):
+        @pl.when(r + AHEAD < n_req + 1)
+        def _():
+            gather_near(r + AHEAD, 0)
+
+    def gather_relay(i):
         for way, side in enumerate((1, -1)):
             src_dev = chip(-2 * side)
-            arrived(r, src_dev)
+            arrived(i, src_dev)
 
             @pl.when(core == way)
             def _(side=side, src_dev=src_dev):
-                q_copy(r, 6, src_dev, 2 * side).start()
-            q_copy(r, 4 + way, src_dev, side).start()
-            cross_copy(r, 1 + way, src_dev).start()
+                q_copy(i, 6, src_dev, 2 * side).start()
+            q_copy(i, 4 + way, src_dev, side).start()
+            cross_copy(i, 1 + way, src_dev).start()
         for way, side in enumerate((1, -1)):
-            arrived(r, chip(side))
-            cross_copy(r, 3 + way, chip(side)).start()
-
-    def gather_far(r):
+            arrived(i, chip(side))
+            cross_copy(i, 3 + way, chip(side)).start()
+
+    def gather_far(i):
         for slot, off in ((5, 3), (6, -3), (7, 4)):
-            arrived(r, chip(off))
-            cross_copy(r, slot, chip(off)).start()
+            arrived(i, chip(off))
+            cross_copy(i, slot, chip(off)).start()
+
+    def first_too(body):
+        def run(r):
+            @pl.when(r == 0)
+            def _():
+                body(0)
+            body(r + 1)
+        return run
 
     def attend(r):
         def from_partner(d, carry):
-            arrived(r, d * 2 + 1 - core)
+            arrived(r + 1, d * 2 + 1 - core)
             return carry
         lax.fori_loop(0, nz, from_partner, 0)
+
+        @pl.when(r == 0)
+        def _():
+            for d in range(nz):
+                arrived(0, d * 2 + 1 - core)
         pltpu.make_async_copy(c_hbm.at[r], c_buf.at[r], c_sem.at[r]).wait()
         pltpu.make_async_copy(k_hbm.at[r], k_buf.at[r], k_sem.at[r]).wait()
-        q = q_all[r].reshape(heads, latent + LANES)
-        q_lat = q[:, :latent].astype(jnp.bfloat16)
-        q_rope = q[:, latent:latent + rope_dim].astype(jnp.bfloat16)
+        q_lat = q_all[r + 1].reshape(heads, latent).astype(jnp.bfloat16)
+        pair_cols = pl.ds(pl.multiple_of((r // 2) * LANES, LANES), LANES)
+        q_rope = q_all[0, :, :, pair_cols].reshape(heads, LANES)
+        q_rope = jnp.where(r % 2 == 0, q_rope[:, :rope_dim], q_rope[:, rope_dim:]).astype(jnp.bfloat16)
         n = ctx_ref[r]
         base = me * t_dev
         step = 512
@@ -273,7 +301,7 @@
         acc, _, mass = merge([mine[r, z], last[r, 0], last[r, 1]], latent)
         o_lat[r] = acc / mass
 
-    lane = lax.broadcasted_iota(jnp.int32, (n_req, per, latent + LANES), 2)
+    lane = lax.broadcasted_iota(jnp.int32, (n_req, per, wide_row), 2)
     empty = jnp.where(jnp.logical_and(lane >= latent, lane < latent + LANES // 2), LOWEST, 0.0)
     for side in range(2):
         @pl.when(core != side)
@@ -288,25 +316,28 @@
             def _():
                 body(r)
 
-        at_slot(FAR_TURN, gather_far)
-        at_slot(RELAY_TURN, gather_relay)
-        at_slot(turn + 6, finish)
-        at_slot(turn + 4, reduce_relay)
+        at_slot(FAR_TURN, first_too(gather_far))
+        at_slot(RELAY_TURN, first_too(gather_relay))
+        at_slot(0, gather_later)
+        at_slot(turn + 2 * RS_TURN + 2, finish)
+        at_slot(turn + RS_TURN + 2, reduce_relay)
         at_slot(turn + 2, reduce_pair)
 
         def compute(r):
             attend(r)
             cross_sum(r).start()
+
+            @pl.when(r == n_req - 1)
+            def _():
+                wait_uv.wait()
+                by_head(uv_buf, uv_heads)
         at_slot(turn, compute)
         return carry
 
-    def near(r, carry):
-        gather_near(r)
-        return carry
-    lax.fori_loop(0, n_req, near, 0)
+    lax.fori_loop(0, AHEAD, gather_near, 0)
     new_entry()
     turn = FAR_TURN + 1
-    lax.fori_loop(0, n_req + turn + 6, slot, 0)
+    lax.fori_loop(0, n_req + turn + 2 * RS_TURN + 2, slot, 0)
 
     o_heads = []
     for h in range(per):
@@ -348,11 +379,15 @@
         piece_copy(off).wait_send()
         spread(off).wait_send()
 
+    def drain_q(i, carry):
+        for sem in range(7):
+            q_copy(i, sem, me, 1).wait_send()
+        for slot_x in range(nz):
+            cross_copy(i, slot_x, me).wait_send()
+        return carry
+    lax.fori_loop(0, n_req + 1, drain_q, 0)
+
     def drain(r, carry):
-        for sem in range(7):
-            q_copy(r, sem, me, 1).wait_send()
-        for slot_x in range(nz):
-            cross_copy(r, slot_x, me).wait_send()
         cross_sum(r).wait_send()
         for sem in range(4):
             hold_copy(r, sem).wait_send()
@@ -388,7 +423,7 @@
         scratch_shapes=[
             pltpu.VMEM((n_req, t_dev, latent), bf16),
             pltpu.VMEM((n_req, rope_dim, t_dev), bf16),
-            pltpu.VMEM((n_req, n_dev, per, width), f32),
+            pltpu.VMEM((n_req + 1, n_dev, per, latent), f32),
             pltpu.VMEM((heads, t_dev), f32),
             pltpu.VMEM((n_req, nz, 2, per, width), f32),
             pltpu.VMEM((n_req, nz, per, width), f32),
@@ -405,7 +440,8 @@
             pltpu.VMEM((per, latent, nope_dim), bf16),
             pltpu.VMEM((per, latent, v_dim), bf16),
             pltpu.VMEM((2, n_req, q_lora // 2), f32),
-            pltpu.VMEM((n_req, per, width), f32),
+            pltpu.VMEM((n_req + 1, per, latent), f32),
+            pltpu.VMEM((n_req, per, LANES), f32),
             pltpu.VMEM((n_req, latent), f32),
             pltpu.VMEM((n_req, rope_dim), f32),
             pltpu.VMEM((n_req, per, latent), f32),
@@ -414,9 +450,9 @@
             pltpu.VMEM((2, n_req, d_model // nz), f32),
             dma((n_req,)),
             dma((n_req,)),
-            dma((n_req, n_dev)),
-            dma((n_req, 7)),
-            dma((n_req, nz)),
+            dma((n_req + 1, n_dev)),
+            dma((n_req + 1, 7)),
+            dma((n_req + 1, nz)),
             dma((n_req,)),
             dma((n_req,)),
             dma((n_req, 5)),
@@ -429,7 +465,21 @@
         ],
         compiler_params=pltpu.CompilerParams(collective_id=0, has_side_effects=True, vmem_limit_bytes=67_000_000),
         name='decode_group',
-    )(ctx_len, x, g_q.reshape(1, -1), g_kv.reshape(1, -1), cos_tab, sin_tab, w_dq, w_uq, w_dkv_t, w_uk, w_uv, w_o, cache_c, cache_krt)
+    )(ctx_len, x, g_q, g_kv, cos_tab, sin_tab, w_dq, w_uq, w_dkv_t, w_uk, w_uv, w_o, cache_c, cache_krt)
+
+
+def emit_kernel(attn_ref, x_ref, c_ref, k_ref, out_ref, cnew_ref, knew_ref):
+    out_ref[...] = (x_ref[...].astype(jnp.float32) + attn_ref[...]).astype(out_ref.dtype)
+    cnew_ref[...] = c_ref[...]
+    knew_ref[...] = k_ref[...]
+
+
+def emit(attn_out, x, c_new, kr_new):
+    return pl.pallas_call(
+        emit_kernel,
+        out_shape=tuple(jax.ShapeDtypeStruct(a.shape, x.dtype) for a in (x, c_new, kr_new)),
+        name='emit',
+    )(attn_out, x, c_new, kr_new)
 
 
 def solution(mesh):
@@ -439,11 +489,9 @@
         rope_dim = cache_kr.shape[2]
         scale = (w_uk.shape[2] + rope_dim) ** -0.5
         cos_tab, sin_tab = rope_tables(ctx_len, rope_dim)
-        cos_tab = jnp.concatenate([cos_tab, cos_tab], axis=1)
-        sin_tab = jnp.concatenate([-sin_tab, sin_tab], axis=1)
         attn_out, c_new, kr_new = decode_group(nz, ctx_len, x, g_q, g_kv, cos_tab, sin_tab, w_dq, w_uq, w_dkv.T, w_uk, w_uv, w_o,
                                                cache_c, cache_kr.transpose(0, 2, 1), scale)
-        return (x.astype(jnp.float32) + attn_out).astype(jnp.bfloat16), c_new, kr_new
+        return emit(attn_out, x, c_new, kr_new)
 
     spec_rows = P('dp', None)
     spec_cache = P('dp', 'cp', None)

time: 90 us -> 85 us (0.944)
  local copies, waits for them, and re-layouts: 3.84 us -> 0 us
  other arithmetic: 3.07 us -> 1.39 us
    unnamed x2 -> x0, local copies, waits for them, and re-layouts: 2.54 us -> none
    convert_element_type x1 -> x0, other arithmetic: 1.62 us -> none  [decode_step(): (x.astype(jnp.float32) + attn_out).astype(jnp.bfloat16)]
    pallas_call x0 -> x1, Pallas kernels: none -> 1.62 us  [emit(): pl.pallas_call(emit_kernel, out_shape=tuple((jax.ShapeDtypeStruct(a.shape...]
    reshape x1 -> x0, local copies, waits for them, and re-layouts: 1.3 us -> none  [decode_group(): g_q.reshape(1, -1)]
    pallas_call x1, Pallas kernels: 82.2 us -> 81.2 us  [decode_group(): pl.pallas_call(functools.partial(decode_kernel, nz, scale), out_shape=(ja...]
where the time goes in v3:
time: 85 us; the launch traced here: 84.8 us
  Pallas kernels  82.8 us (97%)
  other arithmetic  1.39 us (2%)
    pallas_call x1, Pallas kernels, decode_group(): pl.pallas_call(functools.partial(decode_kernel, nz, scale), out_shape=(ja...  81.2 us

profile of v3, /device:TPU:21, one launch (start us, length us, event | category | flops | bytes accessed | tf_op | source)
XLA Modules:
  0.0 84.8 jit_solution(13982320660260825083)
XLA Ops:
  0.6 0.7 convert_element_type.10
  1.3 0.7 negate_select_fusion
  2.0 81.2 %decode_group.1 = (f32[8,5120]{1,0:T(8,128)}, bf16[8,512]{1,0:T(8,128)(2,1)}, bf16[8,64]{1,0:T(8,128)(2,1)}) custom-call(s32[8]{0:T(128)} %ctx_ref.1, bf16[8,5120]{1,0:T(8,128)(2,1)} %x_ref.3, f32[1536]{0:T(1024)} %gq_ref.1, f32[512]{0:T(512)} %gkv_ref.1, f32[8,64]{1,0:T(8,128)} %get-tuple-element.10.cos_ref, f32[8,64]{1,0:T(8,128)} %get-tuple-element.9.sin_ref, ...), custom_call_target="tpu_custom_call" | custom-call | tf_op jit(solution)/shard_map/decode_group/pallas_call | solution.py:416
  83.2 1.6 %emit.1 = (bf16[8,5120]{1,0:T(8,128)(2,1)}, bf16[8,512]{1,0:T(8,128)(2,1)}, bf16[8,64]{1,0:T(8,128)(2,1)}) custom-call(f32[8,5120]{1,0:T(8,128)} %get-tuple-element.6.attn_ref, bf16[8,5120]{1,0:T(8,128)(2,1)} %x_ref.3, bf16[8,512]{1,0:T(8,128)(2,1)} %get-tuple-element.7.c_ref, bf16[8,64]{1,0:T(8,128)(2,1)} %get-tuple-element.8.k_ref), custom_call_target="tpu_custom_call" | custom-call | tf_op jit(solution)/shard_map/emit/pallas_call | solution.py:478
  (2 shorter events, 0.0 us)

commit v4 on v3

--- a/solution.py
+++ b/solution.py
@@ -10,10 +10,10 @@
 NORM_EPS = 1e-6
 ROPE_THETA = 10000.0
 LANES = 128
-AHEAD = 3
+AHEAD = 9
 RS_TURN = 3
 RELAY_TURN = 2
-FAR_TURN = 4
+FAR_TURN = 6
 LOWEST = float(jnp.finfo(jnp.float32).min)
 MESH = pl.DeviceIdType.MESH
 
@@ -334,7 +334,7 @@
         at_slot(turn, compute)
         return carry
 
-    lax.fori_loop(0, AHEAD, gather_near, 0)
+    lax.fori_loop(0, min(AHEAD, n_req + 1), gather_near, 0)
     new_entry()
     turn = FAR_TURN + 1
     lax.fori_loop(0, n_req + turn + 2 * RS_TURN + 2, slot, 0)

time: 85 us -> 83.7 us (0.985)
  Pallas kernels: 82.8 us -> 81.5 us
    pallas_call x1, Pallas kernels: 81.2 us -> 79.9 us  [decode_group(): pl.pallas_call(functools.partial(decode_kernel, nz, scale), out_shape=(ja...]
where the time goes in v4:
time: 83.7 us; the launch traced here: 83.5 us
  Pallas kernels  81.5 us (97%)
  other arithmetic  1.39 us (2%)
    pallas_call x1, Pallas kernels, decode_group(): pl.pallas_call(functools.partial(decode_kernel, nz, scale), out_shape=(ja...  79.9 us

profile of v4, /device:TPU:21, one launch (start us, length us, event | category | flops | bytes accessed | tf_op | source)
XLA Modules:
  0.0 83.5 jit_solution(3131844058579014)
XLA Ops:
  0.6 0.7 convert_element_type.10
  1.3 0.7 negate_select_fusion
  2.0 79.9 %decode_group.1 = (f32[8,5120]{1,0:T(8,128)}, bf16[8,512]{1,0:T(8,128)(2,1)}, bf16[8,64]{1,0:T(8,128)(2,1)}) custom-call(s32[8]{0:T(128)} %ctx_ref.1, bf16[8,5120]{1,0:T(8,128)(2,1)} %x_ref.3, f32[1536]{0:T(1024)} %gq_ref.1, f32[512]{0:T(512)} %gkv_ref.1, f32[8,64]{1,0:T(8,128)} %get-tuple-element.10.cos_ref, f32[8,64]{1,0:T(8,128)} %get-tuple-element.9.sin_ref, ...), custom_call_target="tpu_custom_call" | custom-call | tf_op jit(solution)/shard_map/decode_group/pallas_call | solution.py:416
  81.9 1.6 %emit.1 = (bf16[8,5120]{1,0:T(8,128)(2,1)}, bf16[8,512]{1,0:T(8,128)(2,1)}, bf16[8,64]{1,0:T(8,128)(2,1)}) custom-call(f32[8,5120]{1,0:T(8,128)} %get-tuple-element.6.attn_ref, bf16[8,5120]{1,0:T(8,128)(2,1)} %x_ref.3, bf16[8,512]{1,0:T(8,128)(2,1)} %get-tuple-element.7.c_ref, bf16[8,64]{1,0:T(8,128)(2,1)} %get-tuple-element.8.k_ref), custom_call_target="tpu_custom_call" | custom-call | tf_op jit(solution)/shard_map/emit/pallas_call | solution.py:478
  (2 shorter events, 0.0 us)
